TPU v7x, 32 devices: a whole 2x2x4 slice. The times are simulated.
32 devices in a mesh: dp: 8 (over y, x, core), tensor: 4 (over z).
Axes of the slice: x: 2, y: 2, z: 4, core: 2. Of those that a mesh axis runs over, the one named last changes fastest.
Arguments:
- features: bfloat16 [2048, 1024], P(('dp', 'tensor')), may hold values from -6 to 6
- click: int32 [2048], P(('dp', 'tensor')), may hold values 0 or 1
- convert: int32 [2048], P(('dp', 'tensor')), may hold values 0 or 1
- w1: bfloat16 [1024, 2, 4096], P('dp', None, 'tensor'), may hold values from -0.1875 to 0.1875
- b1: float32 [2, 4096], P(None, 'tensor'), may hold values from -4 to 4
- w2: bfloat16 [2, 4096], P(None, 'tensor'), may hold values from -0.1875 to 0.1875
Outputs:
- sample_loss: float32 [2048], P(('dp', 'tensor'))
- grad_features: bfloat16 [2048, 1024], P(('dp', 'tensor'))
- grad_w1: float32 [1024, 2, 4096], P('dp', None, 'tensor')
- grad_b1: float32 [2, 4096], P(None, 'tensor')
- grad_w2: float32 [2, 4096], P(None, 'tensor')
All inputs are finite; a program needn't handle non-finite values. No bound on the sum of `click` or of `convert` on one device may be relied on, other than what follows from the above.
Results may differ from a plain program's by a relative error of at most 0.025.
Values may be sent and summed in bfloat16 or wider, within the bound.
No kernel may reach another device: no remote copies, remote signals or barrier semaphores. Data moves between devices by JAX's collectives and lax.ppermute only.
A program may use at most 64 MiB of HBM per device.

v0:
```python
import math

import jax
import jax.numpy as jnp
from jax import lax
from jax.sharding import PartitionSpec as P


def sample_loss_fn(logits, click, convert):
    first = logits[:, 0]
    second = logits[:, 1]
    label_y = click.astype(jnp.float32)
    label_z = (click * convert).astype(jnp.float32)
    rest = jnp.log(jax.nn.sigmoid(-first) + jax.nn.sigmoid(first) * jax.nn.sigmoid(-second))
    click_part = label_y * jax.nn.log_sigmoid(first) + (1.0 - label_y) * jax.nn.log_sigmoid(-first)
    both_part = (
        label_z * (jax.nn.log_sigmoid(first) + jax.nn.log_sigmoid(second)) + (1.0 - label_z) * rest
    )
    return -click_part - both_part


def loss_slope(logits, click, convert):
    losses, pullback = jax.vjp(lambda value: sample_loss_fn(value, click, convert), logits)
    return (losses, pullback(jnp.ones_like(losses))[0])


def local(features, click, convert, w1, b1, w2):
    own_count, width = features.shape
    local_units = w1.shape[2]
    total = own_count * lax.axis_size("dp") * lax.axis_size("tensor")
    scale = 1.0 / math.sqrt(total)
    group = lax.all_gather(features, "tensor", axis=0, tiled=True)
    group_count = group.shape[0]
    w2f = w2.astype(jnp.float32)
    full_weights = lax.all_gather(w1, "dp", axis=0, tiled=True)
    w_flat = full_weights.reshape(width, 2 * local_units)
    pre_flat = jnp.dot(group, w_flat, preferred_element_type=jnp.float32)
    pre = pre_flat.reshape(group_count, 2, local_units) + b1[None]
    hidden = jnp.maximum(pre, 0.0).astype(jnp.bfloat16)
    partial_logits = jnp.sum(hidden.astype(jnp.float32) * w2f[None], axis=2)
    logits = lax.psum(partial_logits, "tensor")
    labels = lax.all_gather(jnp.stack([click, convert], axis=1), "tensor", axis=0, tiled=True)
    losses_all, slope = loss_slope(logits, labels[:, 0], labels[:, 1])
    offset = lax.axis_index("tensor") * own_count
    losses = lax.dynamic_slice_in_dim(losses_all, offset, own_count, 0)
    dhidden = jnp.where(pre > 0.0, slope[:, :, None] * w2f[None], 0.0).astype(jnp.bfloat16)
    d_flat = dhidden.reshape(group_count, 2 * local_units)
    partial_rows = jnp.dot(d_flat, w_flat.T, preferred_element_type=jnp.float32)
    grad_features = lax.psum_scatter(
        partial_rows.astype(jnp.bfloat16), "tensor", scatter_dimension=0, tiled=True
    )
    grad_w1 = (
        lax.psum_scatter(
            jnp.dot(group.T, d_flat, preferred_element_type=jnp.float32).reshape(
                w1.shape[0] * lax.axis_size("dp"), 2, local_units
            ),
            "dp",
            scatter_dimension=0,
            tiled=True,
        )
        * scale
    )
    bias_term = jnp.sum(dhidden.astype(jnp.float32), axis=0)
    out_term = jnp.sum(slope[:, :, None] * hidden.astype(jnp.float32), axis=0)
    stacked = jnp.concatenate([bias_term, out_term], axis=0).reshape(4 * local_units)
    summed_share = lax.psum_scatter(stacked, "dp", scatter_dimension=0, tiled=True)
    summed = lax.all_gather(summed_share, "dp", axis=0, tiled=True).reshape(4, local_units)
    return (losses, grad_features, grad_w1, summed[0:2] * scale, summed[2:4] * scale)


def solution(mesh):
    placed = (
        P(("dp", "tensor"), None),
        P(("dp", "tensor")),
        P(("dp", "tensor")),
        P("dp", None, "tensor"),
        P(None, "tensor"),
        P(None, "tensor"),
    )
    return jax.shard_map(
        local,
        mesh=mesh,
        in_specs=placed,
        out_specs=(
            P(("dp", "tensor")),
            P(("dp", "tensor"), None),
            P("dp", None, "tensor"),
            P(None, "tensor"),
            P(None, "tensor"),
        ),
        check_vma=False,
    )
```

profile of v0, /device:TPU:0, one launch (start us, length us, event | category | flops | bytes accessed | tf_op | source)
XLA Modules:
  0.0 247.1 jit_solution(14040047813473934974)
XLA Ops:
  7.2 2.0 copy.19
  9.2 0.7 convert_element_type.35
  9.9 0.7 add_bitcast_fusion
  10.6 12.6 %all-gather = s32[4,64,2]{1,2,0:T(2,128)S(1)} all-gather(s32[1,64,2]{1,2,0:T(2,128)S(1)} %add_bitcast_fusion), channel_id=1, replica_groups=mesh['dp'=8,'tensor'=4] {'tensor'}, dimensions={0}, use_global_device_ids=true | all-gather | bytes 2560 | tf_op jit(solution)/shard_map/all_gather | solution.py:42
  23.3 15.0 %all_gather.13 = bf16[256,1024]{1,0:T(8,128)(2,1)S(1)} all-gather(bf16[64,1024]{1,0:T(8,128)(2,1)} %param.7), channel_id=1, replica_groups=mesh['dp'=8,'tensor'=4] {'tensor'}, dimensions={0}, use_global_device_ids=true | all-gather | bytes 655360 | tf_op jit(solution)/shard_map/all_gather | solution.py:32
  38.3 11.5 %all-gather.4.cloned.1.call-done = bf16[1024,2,1024]{2,0,1:T(8,128)(2,1)} async-done(((bf16[128,2,1024]{2,0,1:T(8,128)(2,1)}), bf16[1024,2,1024]{2,0,1:T(8,128)(2,1)}) %all-gather.4.cloned.1.call-update) | async-done | bytes 4194320 | tf_op jit(solution)/shard_map/all_gather | solution.py:35
  49.8 6.2 %copy.20 = bf16[1024,2,1024]{0,2,1:T(8,128)(2,1)} copy(bf16[1024,2,1024]{2,0,1:T(8,128)(2,1)} %all-gather.4.cloned.1.call-done) | data formatting | bytes 8388608 | tf_op jit(solution)/shard_map/all_gather | solution.py:35
  56.0 3.6 %fusion.2 = (f32[256,2]{0,1:T(2,128)S(1)}, f32[256,2,1024]{2,0,1:T(8,128)S(1)}) fusion(f32[2,1024]{1,0:T(2,128)S(1)} %convert_element_type.35, f32[2,1024]{1,0:T(2,128)S(1)} %copy-done.2, bf16[1024,2,1024]{0,2,1:T(8,128)(2,1)} %copy.20, bf16[256,1024]{1,0:T(8,128)(2,1)S(1)} %all_gather.13), kind=kOutput, calls=%fused_computation.4 | convolution fusion | flops 1076887040 | bytes 6834176 | tf_op jit(solution)/shard_map/dot_general | solution.py:37
  59.6 11.7 %psum.7 = f32[256,2]{0,1:T(2,128)S(1)} all-reduce(f32[256,2]{0,1:T(2,128)S(1)} %get-tuple-element.29), channel_id=1, replica_groups=mesh['dp'=8,'tensor'=4] {'tensor'}, use_global_device_ids=true, to_apply=%region_1.0 | all-reduce | flops 512 | bytes 4096 | tf_op jit(solution)/shard_map/psum | solution.py:41
  71.7 0.8 convert_reduce_fusion
  72.5 0.5 copy.21
  73.1 0.5 copy-done.1
  73.6 4.5 %fusion.34 = f32[2048,1024]{1,0:T(8,128)} fusion(bf16[256,2048]{0,1:T(8,128)(2,1)S(1)} %bitcast.45, bf16[256,1024]{1,0:T(8,128)(2,1)S(1)} %copy-done.1), kind=kOutput, calls=%fused_computation.71 | convolution fusion | flops 1073741824 | bytes 9961472 | tf_op jit(solution)/shard_map/dot_general | solution.py:54
  78.0 13.4 %copy.22 = f32[1024,2,1024]{2,1,0:T(2,128)} copy(f32[1024,2,1024]{0,2,1:T(8,128)} %bitcast.44) | data formatting | bytes 16777216 | tf_op jit(solution)/shard_map/reshape | solution.py:54
  91.5 4.3 %fusion.4 = bf16[256,1024]{1,0:T(8,128)(2,1)} fusion(bf16[1024,2,1024]{2,0,1:T(8,128)(2,1)} %all-gather.4.cloned.1.call-done, f32[256,2]{0,1:T(2,128)S(1)} %pad_add_fusion, f32[2,1024]{1,0:T(2,128)S(1)} %convert_element_type.35, u8[256,1024]{1,0:T(8,128)(4,1)S(1)} %fusion.5), kind=kOutput, calls=%fused_computation.12 | convolution fusion | flops 1077673984 | bytes 4990976 | tf_op jit(solution)/shard_map/dot_general | solution.py:48
  95.8 0.6 dynamic-slice
  97.7 24.1 %all-reduce.3 = f32[4096]{0:T(1024)S(1)} all-reduce(f32[4096]{0:T(1024)S(1)} %bitcast.46), channel_id=4, replica_groups=mesh['dp'=8,'tensor'=4] {'dp'}, use_global_device_ids=true, to_apply=%region_6.8.clone | all-reduce | flops 4096 | bytes 32768
  121.9 9.1 %all-gather.1 = f32[8,1,512]{2,1,0:T(1,128)S(1)} all-gather(f32[1,1,512]{2,1,0:T(1,128)S(1)} %bitcast.47), channel_id=1, replica_groups=mesh['dp'=8,'tensor'=4] {'dp'}, dimensions={0}, use_global_device_ids=true | all-gather | bytes 18432 | tf_op jit(solution)/shard_map/all_gather | solution.py:67
  131.1 0.6 mul.146
  131.7 0.6 mul.148
  132.3 0.6 dynamic_slice.3
  132.9 82.8 %all-reduce.6.cloned.1.call-done = f32[1024,2,1024]{2,1,0:T(2,128)} async-done(((f32[1024,2,1024]{2,1,0:T(2,128)}), f32[1024,2,1024]{2,1,0:T(2,128)}) %all-reduce.6.cloned.1.call-update) | async-done | bytes 8388624
  215.7 2.7 %dynamic-slice_multiply_fusion = f32[128,2,1024]{2,1,0:T(2,128)} fusion(f32[1024,2,1024]{2,1,0:T(2,128)} %all-reduce.6.cloned.1.call-done, u32[]{:T(128)S(6)} %multiply.1), kind=kLoop, calls=%fused_computation.13 | loop fusion | flops 262144 | bytes 2097156 | tf_op jit(solution)/shard_map/mul | solution.py:53
  218.4 22.1 %reduce-scatter.2.cloned.1.call-done = bf16[64,1024]{1,0:T(8,128)(2,1)} async-done(((bf16[256,1024]{1,0:T(8,128)(2,1)}), bf16[64,1024]{1,0:T(8,128)(2,1)}) %reduce-scatter.2.cloned.1.call-update) | async-done | bytes 131088 | tf_op jit(solution)/shard_map/reduce_scatter | solution.py:49
  (24 shorter events, 0.8 us)
Async XLA Ops:
  7.2 42.6 %all-gather.4.cloned.1.call-start = ((), (), s32[]{:S(2)}) async-start(), calls=%async_computation.1 | async-start | bytes 4718592 | tf_op jit(solution)/shard_map/all_gather | solution.py:35
  9.2 206.5 %all-reduce.6.cloned.1.call-start = ((), (), s32[]{:S(2)}) async-start(), calls=%async_computation.3 | async-start | bytes 16777216
  38.3 17.7 %copy-start = (bf16[256,1024]{1,0:T(8,128)(2,1)}, bf16[256,1024]{1,0:T(8,128)(2,1)S(1)}, u32[]{:S(2)}) copy-start(bf16[256,1024]{1,0:T(8,128)(2,1)S(1)} %all_gather.13) | copy-start | bytes 1572868
  38.3 17.7 %copy-start.2 = (f32[2,1024]{1,0:T(2,128)S(1)}, f32[2,1024]{1,0:T(2,128)}, u32[]{:S(2)}) copy-start(f32[2,1024]{1,0:T(2,128)} %param.11) | copy-start | bytes 24580
  72.5 1.0 copy-start.1
  91.4 4.4 %copy-start.3 = (u32[32]{0:T(128)S(1)}, u32[32]{0:T(128)}, u32[]{:S(2)}) copy-start(u32[32]{0:T(128)} %constant.32) | copy-start | bytes 388
  91.4 149.1 %reduce-scatter.2.cloned.1.call-start = ((), (), s32[]{:S(2)}) async-start(), calls=%async_computation.2 | async-start | bytes 655360 | tf_op jit(solution)/shard_map/reduce_scatter | solution.py:49
Sparse Core Ops, SparseCore 0:
  10.4 39.2 all-gather.3
  91.5 124.0 all-reduce.5
  218.5 21.9 reduce-scatter.1
where the time goes:
time: 248 us; the launch traced here: 247 us
  waiting for transfers between devices  116 us (47%)
  blocking collectives  72.5 us (29%)
  local copies, waits for them, and re-layouts  25.2 us (10%)
  between operations  15.1 us (6%)
  matrix products  12.3 us (5%)
  other arithmetic  5.38 us (2%)
    unnamed x4, waiting for transfers between devices  82.8 us
    unnamed x1, blocking collectives  24.1 us
    reduce_scatter x1, waiting for transfers between devices, local(): lax.psum_scatter(partial_rows.astype(jnp.bfloat16), 'tensor', scatter_dim...  22.1 us
    all_gather x1, blocking collectives, local(): group = lax.all_gather(features, 'tensor', axis=0, tiled=True)  15 us
    reshape x1, local copies, waits for them, and re-layouts, local(): jnp.dot(group.T, d_flat, preferred_element_type=jnp.float32)  13.4 us
    all_gather x1, blocking collectives, local(): lax.all_gather(jnp.stack([click, convert], axis=1), 'tensor', axis=0, til...  12.6 us
    psum x1, blocking collectives, local(): logits = lax.psum(partial_logits, 'tensor')  11.7 us
    all_gather x1, waiting for transfers between devices, local(): full_weights = lax.all_gather(w1, 'dp', axis=0, tiled=True)  11.5 us
  transfers between devices with their start and end apart: 3, of which 3 were waited for; matrix products, arithmetic and copies ran while one was open for 4% of the time, Pallas kernels for 0%

commit v1 on v0

--- a/solution.py
+++ b/solution.py
@@ -3,7 +3,13 @@
 import jax
 import jax.numpy as jnp
 from jax import lax
+from jax.experimental import pallas as pl
+from jax.experimental.pallas import tpu as pltpu
 from jax.sharding import PartitionSpec as P
+
+AXES = ("dp", "tensor")
+BF = jnp.bfloat16
+F32 = jnp.float32
 
 
 def sample_loss_fn(logits, click, convert):
@@ -24,7 +30,7 @@
     return (losses, pullback(jnp.ones_like(losses))[0])
 
 
-def local(features, click, convert, w1, b1, w2):
+def general(features, click, convert, w1, b1, w2):
     own_count, width = features.shape
     local_units = w1.shape[2]
     total = own_count * lax.axis_size("dp") * lax.axis_size("tensor")
@@ -49,23 +55,381 @@
     grad_features = lax.psum_scatter(
         partial_rows.astype(jnp.bfloat16), "tensor", scatter_dimension=0, tiled=True
     )
+    partial_w1 = jnp.dot(group.T, d_flat, preferred_element_type=jnp.float32)
     grad_w1 = (
         lax.psum_scatter(
-            jnp.dot(group.T, d_flat, preferred_element_type=jnp.float32).reshape(
-                w1.shape[0] * lax.axis_size("dp"), 2, local_units
-            ),
-            "dp",
-            scatter_dimension=0,
-            tiled=True,
+            partial_w1.reshape(width, 2, local_units), "dp", scatter_dimension=0, tiled=True
         )
         * scale
     )
     bias_term = jnp.sum(dhidden.astype(jnp.float32), axis=0)
     out_term = jnp.sum(slope[:, :, None] * hidden.astype(jnp.float32), axis=0)
-    stacked = jnp.concatenate([bias_term, out_term], axis=0).reshape(4 * local_units)
-    summed_share = lax.psum_scatter(stacked, "dp", scatter_dimension=0, tiled=True)
-    summed = lax.all_gather(summed_share, "dp", axis=0, tiled=True).reshape(4, local_units)
+    summed = lax.psum(jnp.concatenate([bias_term, out_term], axis=0), "dp")
     return (losses, grad_features, grad_w1, summed[0:2] * scale, summed[2:4] * scale)
+
+
+def send(value, mask, tensor_size, dp_size):
+    pairs = [
+        (d * tensor_size + t, (d ^ mask[0]) * tensor_size + (t ^ mask[1]))
+        for d in range(dp_size)
+        for t in range(tensor_size)
+    ]
+    return lax.ppermute(value, AXES, pairs)
+
+
+def call(body, outs, args, flops=0, nbytes=0, vmem=16):
+    spec = pl.BlockSpec(memory_space=pltpu.VMEM)
+    return pl.pallas_call(
+        body,
+        out_shape=[jax.ShapeDtypeStruct(shape, dtype) for shape, dtype in outs],
+        in_specs=[spec] * len(args),
+        out_specs=[spec] * len(outs),
+        compiler_params=pltpu.CompilerParams(vmem_limit_bytes=vmem << 20),
+        cost_estimate=pl.CostEstimate(
+            flops=max(int(flops), 1 << 20), bytes_accessed=int(nbytes), transcendentals=0
+        ),
+    )(*args)
+
+
+def place():
+    me = lax.axis_index("dp")
+    return (lax.div(me, 2), lax.rem(me, 2), lax.axis_index("tensor"))
+
+
+def at(index, size):
+    return pl.ds(pl.multiple_of(index * size, size), size)
+
+
+def mm(a, b):
+    return jnp.dot(a, b, preferred_element_type=F32)
+
+
+def mm_t(a, b):
+    return lax.dot_general(a, b, (((1,), (1,)), ((), ())), preferred_element_type=F32)
+
+
+def with_tail(vec):
+    return jnp.concatenate([vec, vec - vec.astype(BF).astype(F32)], axis=0).astype(BF)
+
+
+def from_tail(tail):
+    tail = tail.astype(F32)
+    return tail[:8] + tail[8:]
+
+
+def join_body(n_t, own, *refs):
+    blocks, out = refs[:n_t], refs[n_t]
+    _, _, z = place()
+    row = lax.broadcasted_iota(jnp.int32, (16, out.shape[1]), 0)
+    labels = jnp.zeros((16, out.shape[1]), F32)
+    for k in range(n_t):
+        where = z ^ k
+        out[at(where, own), :] = blocks[k][:own, :]
+        line = jnp.broadcast_to(blocks[k][own : own + 16, :].astype(F32)[0:1, :], labels.shape)
+        labels = jnp.where(row == where, line, labels)
+    out[n_t * own :, :] = labels.astype(BF)
+
+
+def turn_body(count, pair, mine, theirs, x, lab, *turned):
+    chip, core, _ = place()
+    half = count // 2
+    x[at(core, half), :] = mine[:half, :]
+    x[at(1 - core, half), :] = theirs[:half, :]
+    lab[at(core, 16), :] = mine[half:, :].astype(F32)
+    lab[at(1 - core, 16), :] = theirs[half:, :].astype(F32)
+    for b in range(4):
+        turned[b][...] = x[:, at(chip ^ b, pair)].astype(F32).T.astype(BF)
+
+
+def first_body(pair, x, m0, o0, m1, o1, m2, o2, acc, w_0, w_1, w_2):
+    chip, core, _ = place()
+    rows = pair // 2
+    for w, m, o in ((w_0, m0, o0), (w_1, m1, o1), (w_2, m2, o2)):
+        w[at(core, rows), :] = m[...]
+        w[at(1 - core, rows), :] = o[...]
+    acc[...] = mm(x[:, at(chip, pair)], w_0[...])
+    acc[...] += mm(x[:, at(chip ^ 1, pair)], w_1[...])
+    acc[...] += mm(x[:, at(chip ^ 2, pair)], w_2[...])
+
+
+def last_body(pair, acc, x, m3, o3, bias, out_rows, hidden, logits, w_3):
+    chip, core, _ = place()
+    rows = pair // 2
+    w_3[at(core, rows), :] = m3[...]
+    w_3[at(1 - core, rows), :] = o3[...]
+    pre = acc[...] + mm(x[:, at(chip ^ 3, pair)], w_3[...]) + bias[...]
+    hidden[...] = jnp.maximum(pre, 0.0).astype(BF)
+    logits[...] = mm_t(out_rows[...], hidden[...])[:8]
+
+
+def gate_body(hidden, out_rows, gated):
+    line = jnp.sum(out_rows[...].astype(F32), axis=0, keepdims=True)
+    gated[...] = jnp.where(hidden[...].astype(F32) > 0.0, line, 0.0).astype(BF)
+
+
+def add_body(a, b, out):
+    out[...] = a[...] + b[...]
+
+
+def slope_body(half, pair, a, b, labels, gated, hidden, xt, losses, dh, vec, far0, far1):
+    total = a[...] + b[...]
+    first, second = total[0:1], total[1:2]
+    y, z = labels[0:1], labels[1:2]
+    s_a, s_b = jax.nn.sigmoid(first), jax.nn.sigmoid(second)
+    n_a, n_b = jax.nn.sigmoid(-first), jax.nn.sigmoid(-second)
+    rest = n_a + s_a * n_b
+    log_a, log_b = jax.nn.log_sigmoid(first), jax.nn.log_sigmoid(second)
+    log_na = jax.nn.log_sigmoid(-first)
+    losses[...] = -(y * log_a + (1.0 - y) * log_na) - (
+        z * (log_a + log_b) + (1.0 - z) * jnp.log(rest)
+    )
+    share = (1.0 - z) / rest
+    slope_a = (s_a - y) - (z * n_a - share * (s_a * n_a * s_b))
+    slope_b = -(z * n_b - share * (s_a * s_b * n_b))
+    count = total.shape[1]
+    slopes = jnp.concatenate([slope_a, slope_b, jnp.zeros((6, count), F32)], axis=0)
+    column = slopes.T
+    for t in range(2):
+        cols = slice(t * half, (t + 1) * half)
+        dh[:, cols] = (column[:, t : t + 1] * gated[:, cols].astype(F32)).astype(BF)
+    for t, far in ((0, far0), (1, far1)):
+        far[: pair, :] = mm(xt[...], dh[:, t * half : (t + 1) * half]).astype(BF)
+    bias = mm(jnp.ones((16, count), BF), dh[...])
+    out = mm(with_tail(slopes), hidden[...])
+    out = out[:8] + out[8:]
+    row = lax.broadcasted_iota(jnp.int32, (8, half), 0)
+    for t, far in ((0, far0), (1, far1)):
+        cols = slice(t * half, (t + 1) * half)
+        own = jnp.where(
+            row == 0, bias[:8, cols], jnp.broadcast_to(out[t : t + 1, cols], (8, half))
+        )
+        vec[:, cols] = own
+        far[pair:, :] = with_tail(own)
+
+
+def near_body(half, dh, xt1, xt2, near0, near1):
+    near0[...] = mm(xt1[...], dh[:, :half]).astype(BF)
+    near1[...] = mm(xt2[...], dh[:, half:]).astype(BF)
+
+
+def own_body(half, dh, xt0, xt1, xt2, relay0, relay1, own0, own1):
+    relay0[...] = mm(xt2[...], dh[:, :half])
+    relay1[...] = mm(xt1[...], dh[:, half:])
+    own0[...] = mm(xt0[...], dh[:, :half])
+    own1[...] = mm(xt0[...], dh[:, half:])
+
+
+def relay_body(pair, base, vec, got, out, vec_out):
+    out[:pair, :] = (base[...] + got[:pair, :].astype(F32)).astype(BF)
+    total = vec[...] + from_tail(got[pair:, :])
+    vec_out[...] = total
+    out[pair:, :] = with_tail(total)
+
+
+def final_body(pair, base, near, got, vec, keep, give, vec_out):
+    _, core, _ = place()
+    rows = pair // 2
+    total = vec[...] + from_tail(got[pair:, :])
+    vec_out[...] = total
+    give[rows:, :] = with_tail(total)
+    for which, away in ((core, False), (1 - core, True)):
+        part = at(which, rows)
+        value = base[part, :] + near[part, :].astype(F32) + got[part, :].astype(F32)
+        if away:
+            give[:rows, :] = value.astype(BF)
+        else:
+            keep[...] = value
+
+
+def out_body(half, scale, keep0, keep1, got0, got1, vec0, vec1, grad_w1, grad_b1, grad_w2):
+    _, core, _ = place()
+    rows = keep0.shape[0]
+    here, there = at(core, half), at(1 - core, half)
+    for t, (keep, got, vec) in enumerate(((keep0, got0, vec0), (keep1, got1, vec1))):
+        grad_w1[:, t, here] = keep[...] * scale
+        grad_w1[:, t, there] = got[:rows, :].astype(F32) * scale
+        other = from_tail(got[rows:, :]) * scale
+        mine = vec[...] * scale
+        for row, grad in ((0, grad_b1), (1, grad_w2)):
+            grad[t : t + 1, here] = mine[row : row + 1]
+            grad[t : t + 1, there] = other[row : row + 1]
+
+
+def back_body(pair, dh, w_0, w_1, w_2, w_3, keep, give):
+    chip, core, _ = place()
+    half = dh.shape[0] // 2
+    for b, w in enumerate((w_0, w_1, w_2, w_3)):
+        give[:, at(chip ^ b, pair)] = mm_t(dh[at(1 - core, half), :], w[...]).astype(BF)
+    for b, w in enumerate((w_0, w_1, w_2, w_3)):
+        keep[:, at(chip ^ b, pair)] = mm_t(dh[at(core, half), :], w[...])
+
+
+def spread_body(n_t, own, keep, got, *outs):
+    _, _, z = place()
+    for k in range(n_t):
+        part = at(z ^ k, own)
+        value = keep[part, :] + got[part, :].astype(F32)
+        outs[k][...] = value.astype(outs[k].dtype)
+
+
+def sum_body(*refs):
+    total = refs[0][...]
+    for ref in refs[1:-1]:
+        total = total + ref[...].astype(F32)
+    refs[-1][...] = total.astype(refs[-1].dtype)
+
+
+def cube(features, click, convert, w1, b1, w2):
+    own, width = features.shape
+    rows, towers, units = w1.shape
+    n_dp, n_t = lax.axis_size("dp"), lax.axis_size("tensor")
+    half = units // 2
+    cols = towers * half
+    pair = 2 * rows
+    count = 2 * n_t * own
+    scale = 1.0 / math.sqrt(own * n_dp * n_t)
+    CORE, X, Y = 1, 2, 4
+    _, core, z = place()
+
+    def ex(value, mask):
+        return send(value, mask, n_t, n_dp)
+
+    def part(fn, *static):
+        return lambda *refs: fn(*static, *refs)
+
+    def half_of(which):
+        return lax.dynamic_slice_in_dim(w1, which * half, half, 2).reshape(rows, cols)
+
+    mine, other = half_of(core), half_of(1 - core)
+    label = jnp.concatenate(
+        [
+            jnp.pad(click.astype(BF), (0, 128 - own)),
+            jnp.pad((click * convert).astype(BF), (0, width - 128 - own)),
+        ]
+    )
+    aug = jnp.concatenate([features, jnp.pad(label[None], ((0, 15), (0, 0)))], axis=0)
+
+    x_other = ex(other, (X | CORE, 0))
+    y_mine = ex(mine, (Y, 0))
+    x_mine = ex(mine, (X, 0))
+    y_other = ex(other, (Y | CORE, 0))
+    sib = ex(other, (CORE, 0))
+    zs = [ex(aug, (0, k)) for k in range(1, n_t)]
+    d_mine = ex(y_mine, (X, 0))
+    d_other = ex(x_other, (Y, 0))
+    (core_samples,) = call(part(join_body, n_t, own), [((n_t * own + 16, width), BF)], [aug] + zs)
+    sib_samples = ex(core_samples, (CORE, 0))
+    x, lab, xt0, xt1, xt2, xt3 = call(
+        part(turn_body, count, pair),
+        [((count, width), BF), ((32, width), F32)] + [((pair, count), BF)] * 4,
+        [core_samples, sib_samples],
+    )
+    lab = lab.reshape(2, 16, width)
+    labels = jnp.stack(
+        [lab[:, :n_t, :own].reshape(count), lab[:, :n_t, 128 : 128 + own].reshape(count)]
+    )
+    bias = lax.dynamic_slice_in_dim(b1, core * half, half, 1).reshape(1, cols)
+    w2_half = lax.dynamic_slice_in_dim(w2, core * half, half, 1)
+    out_rows = jnp.concatenate(
+        [
+            jnp.pad(w2_half[t : t + 1], ((0, 0), (t * half, cols - (t + 1) * half)))
+            for t in range(towers)
+        ]
+        + [jnp.zeros((14, cols), BF)],
+        axis=0,
+    )
+
+    acc, w_0, w_1, w_2 = call(
+        part(first_body, pair),
+        [((count, cols), F32)] + [((pair, cols), BF)] * 3,
+        [x, mine, sib, x_mine, x_other, y_mine, y_other],
+        flops=6 * count * pair * cols,
+    )
+    hidden, logits, w_3 = call(
+        part(last_body, pair),
+        [((count, cols), BF), ((8, count), F32), ((pair, cols), BF)],
+        [acc, x, d_mine, d_other, bias, out_rows],
+        flops=2 * count * pair * cols,
+    )
+    (gated,) = call(gate_body, [((count, cols), BF)], [hidden, out_rows], flops=1 << 29)
+
+    def step(a, b):
+        return call(add_body, [((8, count), F32)], [a, b])[0]
+
+    got = ex(logits, (CORE, 0))
+    k = 1
+    while k < n_t:
+        logits = step(logits, got)
+        got = ex(logits, (0, k))
+        k *= 2
+    losses_all, dh, vec, far0, far1 = call(
+        part(slope_body, half, pair),
+        [((1, count), F32), ((count, cols), BF), ((8, cols), F32)]
+        + [((pair + 16, half), BF)] * 2,
+        [logits, got, labels, gated, hidden, xt3],
+        flops=6 * count * pair * cols,
+    )
+    losses = lax.dynamic_slice_in_dim(losses_all[0], (core * n_t + z) * own, own, 0)
+
+    far0 = ex(far0, (X, 0))
+    far1 = ex(far1, (Y, 0))
+    near0, near1 = call(
+        part(near_body, half),
+        [((pair, half), BF)] * 2,
+        [dh, xt1, xt2],
+        flops=2 * count * pair * cols,
+    )
+    near0 = ex(near0, (X, 0))
+    near1 = ex(near1, (Y, 0))
+    base0, base1, own0, own1 = call(
+        part(own_body, half),
+        [((pair, half), F32)] * 4,
+        [dh, xt0, xt1, xt2],
+        flops=4 * count * pair * cols,
+    )
+    keep, give = call(
+        part(back_body, pair),
+        [((count // 2, width), F32), ((count // 2, width), BF)],
+        [dh, w_0, w_1, w_2, w_3],
+        flops=2 * count * width * cols,
+    )
+    got = ex(give, (CORE, 0))
+    blocks = call(
+        part(spread_body, n_t, own),
+        [((own, width), F32)] + [((own, width), BF)] * (n_t - 1),
+        [keep, got],
+    )
+    row_parts = [ex(blocks[k], (0, k)) for k in range(1, n_t)]
+    (grad_features,) = call(sum_body, [((own, width), BF)], [blocks[0]] + row_parts)
+
+    kept = []
+    for t, base, mine_t, far, near, via in (
+        (0, base0, own0, far0, near0, Y),
+        (1, base1, own1, far1, near1, X),
+    ):
+        vec_t = vec[:, t * half : (t + 1) * half]
+        relay, vec_t = call(
+            part(relay_body, pair), [((pair + 16, half), BF), ((8, half), F32)], [base, vec_t, far]
+        )
+        relay = ex(relay, (via, 0))
+        kept.append(
+            call(
+                part(final_body, pair),
+                [((rows, half), F32), ((rows + 16, half), BF), ((8, half), F32)],
+                [mine_t, near, relay, vec_t],
+            )
+        )
+    backs = [ex(kept[t][1], (CORE, 0)) for t in range(towers)]
+    grad_w1, grad_b1, grad_w2 = call(
+        part(out_body, half, scale),
+        [((rows, towers, units), F32), ((towers, units), F32), ((towers, units), F32)],
+        [kept[0][0], kept[1][0], backs[0], backs[1], kept[0][2], kept[1][2]],
+    )
+    return (losses, grad_features, grad_w1, grad_b1, grad_w2)
+
+
+def power_of_two(n):
+    return n & (n - 1) == 0
 
 
 def solution(mesh):
@@ -77,6 +441,7 @@
         P(None, "tensor"),
         P(None, "tensor"),
     )
+    local = cube if mesh.shape["dp"] == 8 and power_of_two(mesh.shape["tensor"]) else general
     return jax.shard_map(
         local,
         mesh=mesh,

time: 248 us -> 92.7 us (0.37)
  blocking collectives: 72.5 us -> 0 us
  waiting for transfers between devices: 116 us -> 54.4 us
  starting transfers between devices: 0.12 us -> 23.9 us
  local copies, waits for them, and re-layouts: 25.2 us -> 3.14 us
  between operations: 15.1 us -> 0.9 us
  matrix products: 12.3 us -> 0 us
  Pallas kernels: 0 us -> 8.37 us
  other arithmetic: 5.38 us -> 1.75 us
    unnamed x4 -> x0, waiting for transfers between devices: 82.8 us -> none
    ppermute x0 -> x26, waiting for transfers between devices: none -> 54.4 us  [send(): return lax.ppermute(value, AXES, pairs)]
    all_gather x3 -> x0, blocking collectives: 36.8 us -> none  [the longest x1 15 us: local(): group = lax.all_gather(features, 'tensor', axis=0, tiled=True)]
    unnamed x1 -> x0, blocking collectives: 24.1 us -> none
    ppermute x0 -> x26, starting transfers between devices: none -> 23.9 us  [send(): return lax.ppermute(value, AXES, pairs)]
    reduce_scatter x1 -> x0, waiting for transfers between devices: 22.1 us -> none  [local(): lax.psum_scatter(partial_rows.astype(jnp.bfloat16), 'tensor', scatter_dim...]
    reshape x1 -> x0, local copies, waits for them, and re-layouts: 13.4 us -> none  [local(): jnp.dot(group.T, d_flat, preferred_element_type=jnp.float32)]
    dot_general x3 -> x0, matrix products: 12.3 us -> none  [the longest x1 4.46 us: local(): jnp.dot(group.T, d_flat, preferred_element_type=jnp.float32)]
  transfers between devices with their start and end apart: 3 -> 26, of which waited for: 3 -> 13; matrix products, arithmetic and copies ran while one was open for 4% -> 3% of each run, Pallas kernels for 0% -> 6%
where the time goes in v1:
time: 92.7 us; the launch traced here: 92.5 us
  waiting for transfers between devices  54.4 us (59%)
  starting transfers between devices  23.9 us (26%)
  Pallas kernels  8.37 us (9%)
  local copies, waits for them, and re-layouts  3.14 us (3%)
  other arithmetic  1.75 us (2%)
    ppermute x26, waiting for transfers between devices, send(): return lax.ppermute(value, AXES, pairs)  54.4 us
    ppermute x26, starting transfers between devices, send(): return lax.ppermute(value, AXES, pairs)  23.9 us
    pallas_call x18, Pallas kernels, call(): pl.pallas_call(body, out_shape=[jax.ShapeDtypeStruct(shape, dtype) for sh...  8.37 us
  transfers between devices with their start and end apart: 26, of which 13 were waited for; matrix products, arithmetic and copies ran while one was open for 3% of the time, Pallas kernels for 6%

profile of v1, /device:TPU:0, one launch (start us, length us, event | category | flops | bytes accessed | tf_op | source)
XLA Modules:
  0.0 92.5 jit_solution(16388213013554051067)
XLA Ops:
  2.3 5.1 %collective-permute-start.2 = (bf16[80,1024]{1,0:T(8,128)(2,1)S(1)}, bf16[80,1024]{1,0:T(8,128)(2,1)S(1)}, u32[]{:S(2)}, u32[]{:S(2)}) collective-permute-start(bf16[80,1024]{1,0:T(8,128)(2,1)S(1)} %fusion.1.refs_0_), channel_id=1, source_target_pairs={{0,3},{1,2},{2,1},{3,0},{4,7},{5,6},{6,5},{7,4},{8,11},{9,10},{10,... | collective-permute-start | bytes 491528 | tf_op jit(solution)/shard_map/ppermute | solution.py:77
  8.1 4.5 %collective-permute-done.2.refs_3_ = bf16[80,1024]{1,0:T(8,128)(2,1)S(1)} collective-permute-done((bf16[80,1024]{1,0:T(8,128)(2,1)S(1)}, bf16[80,1024]{1,0:T(8,128)(2,1)S(1)}, u32[]{:S(2)}, u32[]{:S(2)}) %collective-permute-start.2) | collective-permute-done | bytes 163872 | tf_op jit(solution)/shard_map/ppermute | solution.py:77
  12.6 8.7 %collective-permute-done.1.refs_2_ = bf16[80,1024]{1,0:T(8,128)(2,1)S(1)} collective-permute-done((bf16[80,1024]{1,0:T(8,128)(2,1)S(1)}, bf16[80,1024]{1,0:T(8,128)(2,1)S(1)}, u32[]{:S(2)}, u32[]{:S(2)}) %collective-permute-start.1) | collective-permute-done | bytes 163872 | tf_op jit(solution)/shard_map/ppermute | solution.py:77
  21.5 1.4 %constant_dynamic-slice_fusion.2 = (bf16[128,2,512]{2,1,0:T(2,128)(2,1)S(1)}, bf16[128,2,512]{2,1,0:T(2,128)(2,1)S(1)}) fusion(bf16[128,2,1024]{2,1,0:T(2,128)(2,1)} %param.9, s32[]{:T(128)S(6)} %select_n.12, s32[]{:T(128)S(6)} %select_n.11), kind=kLoop, calls=%fused_computation.20 | loop fusion | bytes 1048584 | tf_op jit(solution)/shard_map/dynamic_slice | solution.py:301
  23.0 1.6 %collective-permute-start.7 = (bf16[128,1024]{1,0:T(8,128)(2,1)S(1)}, bf16[128,1024]{1,0:T(8,128)(2,1)S(1)}, u32[]{:S(2)}, u32[]{:S(2)}) collective-permute-start(bf16[128,1024]{1,0:T(8,128)(2,1)S(1)} %bitcast.11), channel_id=1, source_target_pairs={{0,16},{1,17},{2,18},{3,19},{4,20},{5,21},{6,22},{7,23},{8,24},{9,... | collective-permute-start | bytes 786440 | tf_op jit(solution)/shard_map/ppermute | solution.py:77
  25.3 1.3 %collective-permute-start.6 = (bf16[128,1024]{1,0:T(8,128)(2,1)}, bf16[128,1024]{1,0:T(8,128)(2,1)S(1)}, u32[]{:S(2)}, u32[]{:S(2)}) collective-permute-start(bf16[128,1024]{1,0:T(8,128)(2,1)} %bitcast.5), channel_id=1, source_target_pairs={{0,12},{1,13},{2,14},{3,15},{4,8},{5,9},{6,10},{7,11},{8,4},{9,5},... | collective-permute-start | bytes 786440 | tf_op jit(solution)/shard_map/ppermute | solution.py:77
  27.3 4.9 %collective-permute-done.7.refs_5_ = bf16[128,1024]{1,0:T(8,128)(2,1)S(1)} collective-permute-done((bf16[128,1024]{1,0:T(8,128)(2,1)S(1)}, bf16[128,1024]{1,0:T(8,128)(2,1)S(1)}, u32[]{:S(2)}, u32[]{:S(2)}) %collective-permute-start.7) | collective-permute-done | bytes 262176 | tf_op jit(solution)/shard_map/ppermute | solution.py:77
  32.4 1.3 %collective-permute-done.6.refs_4_ = bf16[128,1024]{1,0:T(8,128)(2,1)S(1)} collective-permute-done((bf16[128,1024]{1,0:T(8,128)(2,1)}, bf16[128,1024]{1,0:T(8,128)(2,1)S(1)}, u32[]{:S(2)}, u32[]{:S(2)}) %collective-permute-start.6) | collective-permute-done | bytes 262176 | tf_op jit(solution)/shard_map/ppermute | solution.py:77
  33.7 1.5 %collective-permute-start.9 = (bf16[128,1024]{1,0:T(8,128)(2,1)S(1)}, bf16[128,1024]{1,0:T(8,128)(2,1)S(1)}, u32[]{:S(2)}, u32[]{:S(2)}) collective-permute-start(bf16[128,1024]{1,0:T(8,128)(2,1)S(1)} %collective-permute-done.7.refs_5_), channel_id=1, source_target_pairs={{0,8},{1,9},{2,10},{3,11},{4,12},{5,13},{6,14},{7,15},{8,0},{9,1},... | collective-permute-start | bytes 786440 | tf_op jit(solution)/shard_map/ppermute | solution.py:77
  36.2 3.9 %collective-permute-done.5.refs_3_ = bf16[128,1024]{1,0:T(8,128)(2,1)S(1)} collective-permute-done((bf16[128,1024]{1,0:T(8,128)(2,1)S(1)}, bf16[128,1024]{1,0:T(8,128)(2,1)S(1)}, u32[]{:S(2)}, u32[]{:S(2)}) %collective-permute-start.5) | collective-permute-done | bytes 262176 | tf_op jit(solution)/shard_map/ppermute | solution.py:77
  41.2 4.1 %collective-permute-done.9.refs_2_ = bf16[128,1024]{1,0:T(8,128)(2,1)S(1)} collective-permute-done((bf16[128,1024]{1,0:T(8,128)(2,1)S(1)}, bf16[128,1024]{1,0:T(8,128)(2,1)S(1)}, u32[]{:S(2)}, u32[]{:S(2)}) %collective-permute-start.9) | collective-permute-done | bytes 262176 | tf_op jit(solution)/shard_map/ppermute | solution.py:77
  47.3 3.7 %collective-permute-done.12.b = f32[8,512]{1,0:T(8,128)S(1)} collective-permute-done((f32[8,512]{1,0:T(8,128)S(1)}, f32[8,512]{1,0:T(8,128)S(1)}, u32[]{:S(2)}, u32[]{:S(2)}) %collective-permute-start.12) | collective-permute-done | bytes 16416 | tf_op jit(solution)/shard_map/ppermute | solution.py:77
  52.3 3.4 %collective-permute-done.13.refs_1_ = f32[8,512]{1,0:T(8,128)S(1)} collective-permute-done((f32[8,512]{1,0:T(8,128)S(1)}, f32[8,512]{1,0:T(8,128)S(1)}, u32[]{:S(2)}, u32[]{:S(2)}) %collective-permute-start.13) | collective-permute-done | bytes 16416 | tf_op jit(solution)/shard_map/ppermute | solution.py:77
  56.7 1.6 %collective-permute-start.19 = (bf16[272,512]{1,0:T(8,128)(2,1)S(1)}, bf16[272,512]{1,0:T(8,128)(2,1)S(1)}, u32[]{:S(2)}, u32[]{:S(2)}) collective-permute-start(bf16[272,512]{1,0:T(8,128)(2,1)S(1)} %get-tuple-element.73), channel_id=1, source_target_pairs={{0,8},{1,9},{2,10},{3,11},{4,12},{5,13},{6,14},{7,15},{8,0},{9,1},... | collective-permute-start | bytes 835592 | tf_op jit(solution)/shard_map/ppermute | solution.py:77
  58.8 1.3 %shard_map.109 = (f32[256,1024]{1,0:T(8,128)S(1)}, bf16[256,1024]{1,0:T(8,128)(2,1)S(1)}) custom-call(bf16[512,1024]{1,0:T(8,128)(2,1)S(1)} %get-tuple-element.55.refs_0_, bf16[256,1024]{1,0:T(8,128)(2,1)S(1)} %copy-done.2, bf16[256,1024]{1,0:T(8,128)(2,1)S(1)} %copy-done.4, bf16[256,1024]{1,0:T(8,128)(2,1)S(1)} %copy-done.6, ...), custom_call_target="tpu_custom_call" | custom-call | flops 1073741824 | tf_op jit(solution)/shard_map/pallas_call | solution.py:82
  60.9 4.0 %collective-permute-done.22.refs_2_ = bf16[272,512]{1,0:T(8,128)(2,1)S(1)} collective-permute-done((bf16[272,512]{1,0:T(8,128)(2,1)S(1)}, bf16[272,512]{1,0:T(8,128)(2,1)S(1)}, u32[]{:S(2)}, u32[]{:S(2)}) %collective-permute-start.22) | collective-permute-done | bytes 278560 | tf_op jit(solution)/shard_map/ppermute | solution.py:77
  66.6 1.6 %collective-permute-start.21 = (bf16[256,512]{1,0:T(8,128)(2,1)S(1)}, bf16[256,512]{1,0:T(8,128)(2,1)S(1)}, u32[]{:S(2)}, u32[]{:S(2)}) collective-permute-start(bf16[256,512]{1,0:T(8,128)(2,1)S(1)} %get-tuple-element.78), channel_id=1, source_target_pairs={{0,16},{1,17},{2,18},{3,19},{4,20},{5,21},{6,22},{7,23},{8,24},{9,... | collective-permute-start | bytes 786440 | tf_op jit(solution)/shard_map/ppermute | solution.py:77
  68.1 1.6 %collective-permute-start.18 = (bf16[256,512]{1,0:T(8,128)(2,1)S(1)}, bf16[256,512]{1,0:T(8,128)(2,1)S(1)}, u32[]{:S(2)}, u32[]{:S(2)}) collective-permute-start(bf16[256,512]{1,0:T(8,128)(2,1)S(1)} %get-tuple-element.70), channel_id=1, source_target_pairs={{0,8},{1,9},{2,10},{3,11},{4,12},{5,13},{6,14},{7,15},{8,0},{9,1},... | collective-permute-start | bytes 786440 | tf_op jit(solution)/shard_map/ppermute | solution.py:77
  69.8 6.6 %collective-permute-done.21.refs_1_ = bf16[256,512]{1,0:T(8,128)(2,1)S(1)} collective-permute-done((bf16[256,512]{1,0:T(8,128)(2,1)S(1)}, bf16[256,512]{1,0:T(8,128)(2,1)S(1)}, u32[]{:S(2)}, u32[]{:S(2)}) %collective-permute-start.21) | collective-permute-done | bytes 262176 | tf_op jit(solution)/shard_map/ppermute | solution.py:77
  77.6 2.8 %collective-permute-start.16 = (bf16[64,1024]{1,0:T(8,128)(2,1)S(1)}, bf16[64,1024]{1,0:T(8,128)(2,1)S(1)}, u32[]{:S(2)}, u32[]{:S(2)}) collective-permute-start(bf16[64,1024]{1,0:T(8,128)(2,1)S(1)} %get-tuple-element.64), channel_id=1, source_target_pairs={{0,2},{1,3},{2,0},{3,1},{4,6},{5,7},{6,4},{7,5},{8,10},{9,11},{10,... | collective-permute-start | bytes 393224 | tf_op jit(solution)/shard_map/ppermute | solution.py:77
  80.4 1.4 %collective-permute-start.17 = (bf16[64,1024]{1,0:T(8,128)(2,1)S(1)}, bf16[64,1024]{1,0:T(8,128)(2,1)S(1)}, u32[]{:S(2)}, u32[]{:S(2)}) collective-permute-start(bf16[64,1024]{1,0:T(8,128)(2,1)S(1)} %get-tuple-element.65), channel_id=1, source_target_pairs={{0,3},{1,2},{2,1},{3,0},{4,7},{5,6},{6,5},{7,4},{8,11},{9,10},{10,... | collective-permute-start | bytes 393224 | tf_op jit(solution)/shard_map/ppermute | solution.py:77
  82.4 2.7 %collective-permute-done.15.refs_1_ = bf16[64,1024]{1,0:T(8,128)(2,1)S(1)} collective-permute-done((bf16[64,1024]{1,0:T(8,128)(2,1)S(1)}, bf16[64,1024]{1,0:T(8,128)(2,1)S(1)}, u32[]{:S(2)}, u32[]{:S(2)}) %collective-permute-start.15) | collective-permute-done | bytes 131104 | tf_op jit(solution)/shard_map/ppermute | solution.py:77
  85.0 5.5 %collective-permute-done.16.refs_2_ = bf16[64,1024]{1,0:T(8,128)(2,1)S(1)} collective-permute-done((bf16[64,1024]{1,0:T(8,128)(2,1)S(1)}, bf16[64,1024]{1,0:T(8,128)(2,1)S(1)}, u32[]{:S(2)}, u32[]{:S(2)}) %collective-permute-start.16) | collective-permute-done | bytes 131104 | tf_op jit(solution)/shard_map/ppermute | solution.py:77
  91.3 1.2 %shard_map.118 = (f32[128,2,1024]{2,1,0:T(2,128)}, f32[2,1024]{1,0:T(2,128)}, f32[2,1024]{1,0:T(2,128)}) custom-call(f32[128,512]{1,0:T(8,128)S(1)} %get-tuple-element.76.refs_0_, f32[128,512]{1,0:T(8,128)S(1)} %get-tuple-element.83.refs_1_, bf16[144,512]{1,0:T(8,128)(2,1)S(1)} %collective-permute-done.24.refs_2_, ...), custom_call_target="tpu_custom_call" | custom-call | flops 1048576 | tf_op jit(solution)/shard_map/pallas_call | solution.py:82
  (81 shorter events, 15.8 us)
Async XLA Ops:
  2.3 10.3 %collective-permute-start.2 = (bf16[80,1024]{1,0:T(8,128)(2,1)S(1)}, bf16[80,1024]{1,0:T(8,128)(2,1)S(1)}, u32[]{:S(2)}, u32[]{:S(2)}) collective-permute-start(bf16[80,1024]{1,0:T(8,128)(2,1)S(1)} %fusion.1.refs_0_), channel_id=1, source_target_pairs={{0,3},{1,2},{2,1},{3,0},{4,7},{5,6},{6,5},{7,4},{8,11},{9,10},{10,... | collective-permute-start | bytes 491528 | tf_op jit(solution)/shard_map/ppermute | solution.py:77
  7.5 13.9 %collective-permute-start.1 = (bf16[80,1024]{1,0:T(8,128)(2,1)S(1)}, bf16[80,1024]{1,0:T(8,128)(2,1)S(1)}, u32[]{:S(2)}, u32[]{:S(2)}) collective-permute-start(bf16[80,1024]{1,0:T(8,128)(2,1)S(1)} %fusion.1.refs_0_), channel_id=1, source_target_pairs={{0,2},{1,3},{2,0},{3,1},{4,6},{5,7},{6,4},{7,5},{8,10},{9,11},{10,... | collective-permute-start | bytes 491528 | tf_op jit(solution)/shard_map/ppermute | solution.py:77
  7.5 13.9 %collective-permute-start = (bf16[80,1024]{1,0:T(8,128)(2,1)S(1)}, bf16[80,1024]{1,0:T(8,128)(2,1)S(1)}, u32[]{:S(2)}, u32[]{:S(2)}) collective-permute-start(bf16[80,1024]{1,0:T(8,128)(2,1)S(1)} %fusion.1.refs_0_), channel_id=1, source_target_pairs={{0,1},{1,0},{2,3},{3,2},{4,5},{5,4},{6,7},{7,6},{8,9},{9,8},{10,11... | collective-permute-start | bytes 491528 | tf_op jit(solution)/shard_map/ppermute | solution.py:77
  21.4 13.8 %collective-permute-start.3 = (bf16[272,1024]{1,0:T(8,128)(2,1)S(1)}, bf16[272,1024]{1,0:T(8,128)(2,1)S(1)}, u32[]{:S(2)}, u32[]{:S(2)}) collective-permute-start(bf16[272,1024]{1,0:T(8,128)(2,1)S(1)} %shard_map.101.refs_0_), channel_id=1, source_target_pairs={{0,4},{1,5},{2,6},{3,7},{4,0},{5,1},{6,2},{7,3},{8,12},{9,13},{10,... | collective-permute-start | bytes 1671176 | tf_op jit(solution)/shard_map/ppermute | solution.py:77
  23.0 9.2 %collective-permute-start.7 = (bf16[128,1024]{1,0:T(8,128)(2,1)S(1)}, bf16[128,1024]{1,0:T(8,128)(2,1)S(1)}, u32[]{:S(2)}, u32[]{:S(2)}) collective-permute-start(bf16[128,1024]{1,0:T(8,128)(2,1)S(1)} %bitcast.11), channel_id=1, source_target_pairs={{0,16},{1,17},{2,18},{3,19},{4,20},{5,21},{6,22},{7,23},{8,24},{9,... | collective-permute-start | bytes 786440 | tf_op jit(solution)/shard_map/ppermute | solution.py:77
  25.3 8.4 %collective-permute-start.6 = (bf16[128,1024]{1,0:T(8,128)(2,1)}, bf16[128,1024]{1,0:T(8,128)(2,1)S(1)}, u32[]{:S(2)}, u32[]{:S(2)}) collective-permute-start(bf16[128,1024]{1,0:T(8,128)(2,1)} %bitcast.5), channel_id=1, source_target_pairs={{0,12},{1,13},{2,14},{3,15},{4,8},{5,9},{6,10},{7,11},{8,4},{9,5},... | collective-permute-start | bytes 786440 | tf_op jit(solution)/shard_map/ppermute | solution.py:77
  26.6 13.5 %collective-permute-start.5 = (bf16[128,1024]{1,0:T(8,128)(2,1)S(1)}, bf16[128,1024]{1,0:T(8,128)(2,1)S(1)}, u32[]{:S(2)}, u32[]{:S(2)}) collective-permute-start(bf16[128,1024]{1,0:T(8,128)(2,1)S(1)} %bitcast.12), channel_id=1, source_target_pairs={{0,8},{1,9},{2,10},{3,11},{4,12},{5,13},{6,14},{7,15},{8,0},{9,1},... | collective-permute-start | bytes 786440 | tf_op jit(solution)/shard_map/ppermute | solution.py:77
  27.1 13.0 %collective-permute-start.8 = (bf16[128,1024]{1,0:T(8,128)(2,1)}, bf16[128,1024]{1,0:T(8,128)(2,1)S(1)}, u32[]{:S(2)}, u32[]{:S(2)}) collective-permute-start(bf16[128,1024]{1,0:T(8,128)(2,1)} %bitcast.5), channel_id=1, source_target_pairs={{0,20},{1,21},{2,22},{3,23},{4,16},{5,17},{6,18},{7,19},{8,28},{9,... | collective-permute-start | bytes 786440 | tf_op jit(solution)/shard_map/ppermute | solution.py:77
  32.2 7.9 %collective-permute-start.4 = (bf16[128,1024]{1,0:T(8,128)(2,1)}, bf16[128,1024]{1,0:T(8,128)(2,1)S(1)}, u32[]{:S(2)}, u32[]{:S(2)}) collective-permute-start(bf16[128,1024]{1,0:T(8,128)(2,1)} %bitcast.5), channel_id=1, source_target_pairs={{0,4},{1,5},{2,6},{3,7},{4,0},{5,1},{6,2},{7,3},{8,12},{9,13},{10,... | collective-permute-start | bytes 786440 | tf_op jit(solution)/shard_map/ppermute | solution.py:77
  33.7 11.6 %collective-permute-start.9 = (bf16[128,1024]{1,0:T(8,128)(2,1)S(1)}, bf16[128,1024]{1,0:T(8,128)(2,1)S(1)}, u32[]{:S(2)}, u32[]{:S(2)}) collective-permute-start(bf16[128,1024]{1,0:T(8,128)(2,1)S(1)} %collective-permute-done.7.refs_5_), channel_id=1, source_target_pairs={{0,8},{1,9},{2,10},{3,11},{4,12},{5,13},{6,14},{7,15},{8,0},{9,1},... | collective-permute-start | bytes 786440 | tf_op jit(solution)/shard_map/ppermute | solution.py:77
  35.2 10.1 %collective-permute-start.10 = (bf16[128,1024]{1,0:T(8,128)(2,1)S(1)}, bf16[128,1024]{1,0:T(8,128)(2,1)S(1)}, u32[]{:S(2)}, u32[]{:S(2)}) collective-permute-start(bf16[128,1024]{1,0:T(8,128)(2,1)S(1)} %collective-permute-done.6.refs_4_), channel_id=1, source_target_pairs={{0,16},{1,17},{2,18},{3,19},{4,20},{5,21},{6,22},{7,23},{8,24},{9,... | collective-permute-start | bytes 786440 | tf_op jit(solution)/shard_map/ppermute | solution.py:77
  51.0 4.6 %collective-permute-start.13 = (f32[8,512]{1,0:T(8,128)S(1)}, f32[8,512]{1,0:T(8,128)S(1)}, u32[]{:S(2)}, u32[]{:S(2)}) collective-permute-start(f32[8,512]{1,0:T(8,128)S(1)} %shard_map.106.refs_0_), channel_id=1, source_target_pairs={{0,2},{1,3},{2,0},{3,1},{4,6},{5,7},{6,4},{7,5},{8,10},{9,11},{10,... | collective-permute-start | bytes 49160 | tf_op jit(solution)/shard_map/ppermute | solution.py:77
  56.7 8.8 %collective-permute-start.19 = (bf16[272,512]{1,0:T(8,128)(2,1)S(1)}, bf16[272,512]{1,0:T(8,128)(2,1)S(1)}, u32[]{:S(2)}, u32[]{:S(2)}) collective-permute-start(bf16[272,512]{1,0:T(8,128)(2,1)S(1)} %get-tuple-element.73), channel_id=1, source_target_pairs={{0,8},{1,9},{2,10},{3,11},{4,12},{5,13},{6,14},{7,15},{8,0},{9,1},... | collective-permute-start | bytes 835592 | tf_op jit(solution)/shard_map/ppermute | solution.py:77
  58.3 6.7 %collective-permute-start.22 = (bf16[272,512]{1,0:T(8,128)(2,1)S(1)}, bf16[272,512]{1,0:T(8,128)(2,1)S(1)}, u32[]{:S(2)}, u32[]{:S(2)}) collective-permute-start(bf16[272,512]{1,0:T(8,128)(2,1)S(1)} %get-tuple-element.80), channel_id=1, source_target_pairs={{0,16},{1,17},{2,18},{3,19},{4,20},{5,21},{6,22},{7,23},{8,24},{9,... | collective-permute-start | bytes 835592 | tf_op jit(solution)/shard_map/ppermute | solution.py:77
  60.1 17.1 %collective-permute-start.14 = (bf16[256,1024]{1,0:T(8,128)(2,1)S(1)}, bf16[256,1024]{1,0:T(8,128)(2,1)S(1)}, u32[]{:S(2)}, u32[]{:S(2)}) collective-permute-start(bf16[256,1024]{1,0:T(8,128)(2,1)S(1)} %get-tuple-element.61), channel_id=1, source_target_pairs={{0,4},{1,5},{2,6},{3,7},{4,0},{5,1},{6,2},{7,3},{8,12},{9,13},{10,... | collective-permute-start | bytes 1572872 | tf_op jit(solution)/shard_map/ppermute | solution.py:77
  65.0 11.4 %collective-permute-start.23 = (bf16[272,512]{1,0:T(8,128)(2,1)S(1)}, bf16[272,512]{1,0:T(8,128)(2,1)S(1)}, u32[]{:S(2)}, u32[]{:S(2)}) collective-permute-start(bf16[272,512]{1,0:T(8,128)(2,1)S(1)} %get-tuple-element.81), channel_id=1, source_target_pairs={{0,8},{1,9},{2,10},{3,11},{4,12},{5,13},{6,14},{7,15},{8,0},{9,1},... | collective-permute-start | bytes 835592 | tf_op jit(solution)/shard_map/ppermute | solution.py:77
  65.5 11.1 %collective-permute-start.20 = (bf16[272,512]{1,0:T(8,128)(2,1)S(1)}, bf16[272,512]{1,0:T(8,128)(2,1)S(1)}, u32[]{:S(2)}, u32[]{:S(2)}) collective-permute-start(bf16[272,512]{1,0:T(8,128)(2,1)S(1)} %get-tuple-element.74), channel_id=1, source_target_pairs={{0,16},{1,17},{2,18},{3,19},{4,20},{5,21},{6,22},{7,23},{8,24},{9,... | collective-permute-start | bytes 835592 | tf_op jit(solution)/shard_map/ppermute | solution.py:77
  66.6 9.9 %collective-permute-start.21 = (bf16[256,512]{1,0:T(8,128)(2,1)S(1)}, bf16[256,512]{1,0:T(8,128)(2,1)S(1)}, u32[]{:S(2)}, u32[]{:S(2)}) collective-permute-start(bf16[256,512]{1,0:T(8,128)(2,1)S(1)} %get-tuple-element.78), channel_id=1, source_target_pairs={{0,16},{1,17},{2,18},{3,19},{4,20},{5,21},{6,22},{7,23},{8,24},{9,... | collective-permute-start | bytes 786440 | tf_op jit(solution)/shard_map/ppermute | solution.py:77
  68.1 8.4 %collective-permute-start.18 = (bf16[256,512]{1,0:T(8,128)(2,1)S(1)}, bf16[256,512]{1,0:T(8,128)(2,1)S(1)}, u32[]{:S(2)}, u32[]{:S(2)}) collective-permute-start(bf16[256,512]{1,0:T(8,128)(2,1)S(1)} %get-tuple-element.70), channel_id=1, source_target_pairs={{0,8},{1,9},{2,10},{3,11},{4,12},{5,13},{6,14},{7,15},{8,0},{9,1},... | collective-permute-start | bytes 786440 | tf_op jit(solution)/shard_map/ppermute | solution.py:77
  76.5 14.7 %collective-permute-start.25 = (bf16[144,512]{1,0:T(8,128)(2,1)S(1)}, bf16[144,512]{1,0:T(8,128)(2,1)S(1)}, u32[]{:S(2)}, u32[]{:S(2)}) collective-permute-start(bf16[144,512]{1,0:T(8,128)(2,1)S(1)} %get-tuple-element.85), channel_id=1, source_target_pairs={{0,4},{1,5},{2,6},{3,7},{4,0},{5,1},{6,2},{7,3},{8,12},{9,13},{10,... | collective-permute-start | bytes 442376 | tf_op jit(solution)/shard_map/ppermute | solution.py:77
  76.7 14.5 %collective-permute-start.24 = (bf16[144,512]{1,0:T(8,128)(2,1)S(1)}, bf16[144,512]{1,0:T(8,128)(2,1)S(1)}, u32[]{:S(2)}, u32[]{:S(2)}) collective-permute-start(bf16[144,512]{1,0:T(8,128)(2,1)S(1)} %get-tuple-element.84), channel_id=1, source_target_pairs={{0,4},{1,5},{2,6},{3,7},{4,0},{5,1},{6,2},{7,3},{8,12},{9,13},{10,... | collective-permute-start | bytes 442376 | tf_op jit(solution)/shard_map/ppermute | solution.py:77
  77.3 7.7 %collective-permute-start.15 = (bf16[64,1024]{1,0:T(8,128)(2,1)S(1)}, bf16[64,1024]{1,0:T(8,128)(2,1)S(1)}, u32[]{:S(2)}, u32[]{:S(2)}) collective-permute-start(bf16[64,1024]{1,0:T(8,128)(2,1)S(1)} %get-tuple-element.63), channel_id=1, source_target_pairs={{0,1},{1,0},{2,3},{3,2},{4,5},{5,4},{6,7},{7,6},{8,9},{9,8},{10,11... | collective-permute-start | bytes 393224 | tf_op jit(solution)/shard_map/ppermute | solution.py:77
  77.6 12.9 %collective-permute-start.16 = (bf16[64,1024]{1,0:T(8,128)(2,1)S(1)}, bf16[64,1024]{1,0:T(8,128)(2,1)S(1)}, u32[]{:S(2)}, u32[]{:S(2)}) collective-permute-start(bf16[64,1024]{1,0:T(8,128)(2,1)S(1)} %get-tuple-element.64), channel_id=1, source_target_pairs={{0,2},{1,3},{2,0},{3,1},{4,6},{5,7},{6,4},{7,5},{8,10},{9,11},{10,... | collective-permute-start | bytes 393224 | tf_op jit(solution)/shard_map/ppermute | solution.py:77
  80.4 10.1 %collective-permute-start.17 = (bf16[64,1024]{1,0:T(8,128)(2,1)S(1)}, bf16[64,1024]{1,0:T(8,128)(2,1)S(1)}, u32[]{:S(2)}, u32[]{:S(2)}) collective-permute-start(bf16[64,1024]{1,0:T(8,128)(2,1)S(1)} %get-tuple-element.65), channel_id=1, source_target_pairs={{0,3},{1,2},{2,1},{3,0},{4,7},{5,6},{6,5},{7,4},{8,11},{9,10},{10,... | collective-permute-start | bytes 393224 | tf_op jit(solution)/shard_map/ppermute | solution.py:77
  (10 other events, 98.2 us)
